TPU v7x, 32 devices: a whole 2x2x4 slice. The times are simulated.
32 devices in a mesh: cand: 4 (over y, core), tensor: 8 (over z, x).
Axes of the slice: x: 2, y: 2, z: 4, core: 2. Of those that a mesh axis runs over, the one named last changes fastest.
Arguments:
- states: bfloat16 [512, 3584], P('cand'), may hold values from -60 to 60
- targets: int32 [512], replicated, may hold values from 0 to 131071
- loss_mask: int32 [512], P('cand'), may hold values 0 or 1
- cand_of: int32 [4], replicated, may hold values from 0 to 3
- lambdas: float32 [4], replicated, may hold values from 0.2 to 1
- base_q: bfloat16 [3584, 4096], P('cand', 'tensor'), may hold values from -0.09375 to 0.09375
- delta_q: bfloat16 [2, 3584, 4096], P(None, 'cand', 'tensor'), may hold values from -0.046875 to 0.046875
- base_k: bfloat16 [3584, 2048], P('cand'), may hold values from -0.09375 to 0.09375
- delta_k: bfloat16 [2, 3584, 2048], P(None, 'cand'), may hold values from -0.046875 to 0.046875
- base_v: bfloat16 [3584, 2048], P('cand'), may hold values from -0.09375 to 0.09375
- delta_v: bfloat16 [2, 3584, 2048], P(None, 'cand'), may hold values from -0.046875 to 0.046875
- base_o: bfloat16 [4096, 3584], P('tensor', 'cand'), may hold values from -0.09375 to 0.09375
- delta_o: bfloat16 [2, 4096, 3584], P(None, 'tensor', 'cand'), may hold values from -0.046875 to 0.046875
- pre_gain: float32 [3584], replicated, may hold values from 0.5 to 2
- post_gain: float32 [3584], replicated, may hold values from 0.5 to 2
- final_gain: float32 [3584], replicated, may hold values from 0.5 to 2
- unembed: bfloat16 [3584, 131072], P(None, ('cand', 'tensor')), may hold values from -0.3125 to 0.3125
Outputs:
- token_loss: float32 [512], P('cand')
- cand_loss: float32 [4], replicated
All inputs are finite; a program needn't handle non-finite values. No bound on the sum of `loss_mask` on one device may be relied on, other than what follows from the above.
Results may differ from a plain program's by a relative error of at most 0.002.
Values may be sent and summed in bfloat16 or wider, within the bound.
No kernel may reach another device: no remote copies, remote signals or barrier semaphores. Data moves between devices by JAX's collectives and lax.ppermute only.
A program may use at most 128 MiB of HBM per device.

v0:
```python
import math
import jax
import jax.numpy as jnp
from jax import lax
from jax.sharding import PartitionSpec as P

KV = 8
HEAD_SIZE = 256
CANDS = 4


def root_norm(entries, scale_gain):
    mean_square = jnp.mean(entries * entries, axis=-1, keepdims=True)
    return entries * lax.rsqrt(mean_square + 1e-06) * scale_gain


def rotate_pairs(entries, length):
    half_width = entries.shape[-1] // 2
    positions = jnp.arange(length).astype(jnp.float32)
    frequency = jnp.exp(
        -math.log(10000.0) * jnp.arange(half_width).astype(jnp.float32) * 2.0 / entries.shape[-1]
    )
    angles = positions[:, None] * frequency[None, :]
    cosine = jnp.cos(angles)[:, None, :]
    sine_part = jnp.sin(angles)[:, None, :]
    first = entries[..., :half_width]
    second = entries[..., half_width:]
    return jnp.concatenate(
        [first * cosine - second * sine_part, second * cosine + first * sine_part], axis=-1
    )


def task_total(delta):
    return jnp.sum(delta.astype(jnp.float32), axis=0).astype(jnp.bfloat16)


def merge_weights(base, total, mixing):
    return (base.astype(jnp.float32) + mixing * total.astype(jnp.float32)).astype(jnp.bfloat16)


def on_device(
    states,
    targets,
    loss_mask,
    cand_of,
    lambdas,
    base_q,
    delta_q,
    base_k,
    delta_k,
    base_v,
    delta_v,
    base_o,
    delta_o,
    pre_gain,
    post_gain,
    final_gain,
    unembed,
):
    cand_id = lax.axis_index("cand")
    tensor_id = lax.axis_index("tensor")
    tensor_count = lax.axis_size("tensor")
    chosen = cand_of[cand_id]
    mixing = lambdas[chosen]
    group_size = tensor_count // KV
    head_start = tensor_id // group_size * HEAD_SIZE
    own_base_k = lax.dynamic_slice_in_dim(base_k, head_start, HEAD_SIZE, 1)
    own_base_v = lax.dynamic_slice_in_dim(base_v, head_start, HEAD_SIZE, 1)
    own_delta_k = lax.dynamic_slice_in_dim(delta_k, head_start, HEAD_SIZE, 2)
    own_delta_v = lax.dynamic_slice_in_dim(delta_v, head_start, HEAD_SIZE, 2)
    summed = [task_total(delta) for delta in (delta_q, own_delta_k, own_delta_v, delta_o)]
    pieces = (
        lax.all_gather(base_q, "cand", axis=0, tiled=True),
        lax.all_gather(own_base_k, "cand", axis=0, tiled=True),
        lax.all_gather(own_base_v, "cand", axis=0, tiled=True),
        lax.all_gather(base_o, "cand", axis=1, tiled=True),
        lax.all_gather(summed[0], "cand", axis=0, tiled=True),
        lax.all_gather(summed[1], "cand", axis=0, tiled=True),
        lax.all_gather(summed[2], "cand", axis=0, tiled=True),
        lax.all_gather(summed[3], "cand", axis=1, tiled=True),
    )
    base_parts = pieces[:4]
    task_parts = pieces[4:]
    w_query = merge_weights(base_parts[0], task_parts[0], mixing)
    w_key = merge_weights(base_parts[1], task_parts[1], mixing)
    w_value = merge_weights(base_parts[2], task_parts[2], mixing)
    w_out = merge_weights(base_parts[3], task_parts[3], mixing)
    length = states.shape[0]
    stream = states.astype(jnp.float32)
    normed = root_norm(stream, pre_gain).astype(jnp.bfloat16)
    query_rows = jnp.dot(normed, w_query, preferred_element_type=jnp.float32).reshape(
        length, -1, HEAD_SIZE
    )
    query_rows = rotate_pairs(query_rows, length).astype(jnp.bfloat16)
    key_full = jnp.dot(normed, w_key, preferred_element_type=jnp.float32).astype(jnp.bfloat16)
    value_full = jnp.dot(normed, w_value, preferred_element_type=jnp.float32).astype(jnp.bfloat16)
    key_matrix = rotate_pairs(
        key_full.astype(jnp.float32).reshape(length, 1, HEAD_SIZE), length
    ).astype(jnp.bfloat16)[:, 0, :]
    attention_scores = jnp.einsum(
        "lhd,md->hlm", query_rows, key_matrix, preferred_element_type=jnp.float32
    ) * HEAD_SIZE ** (-0.5)
    attention_scores = 50.0 * jnp.tanh(attention_scores / 50.0)
    causal = jnp.arange(length)[:, None] >= jnp.arange(length)[None, :]
    weights = jnp.where(causal[None, :, :], jnp.exp(attention_scores), 0.0)
    attention_probs = (weights / jnp.sum(weights, axis=-1, keepdims=True)).astype(jnp.bfloat16)
    context_rows = jnp.einsum(
        "hlm,md->lhd", attention_probs, value_full, preferred_element_type=jnp.float32
    )
    context_rows = context_rows.astype(jnp.bfloat16).reshape(length, -1)
    partial_value = jnp.dot(context_rows, w_out, preferred_element_type=jnp.float32)
    vocab_width = unembed.shape[1]
    vocab_start = (cand_id * tensor_count + tensor_id) * vocab_width
    vocab_index = jnp.arange(vocab_width)
    attended = lax.psum(partial_value, "tensor")
    final_rows = root_norm(stream + root_norm(attended, post_gain), final_gain).astype(jnp.bfloat16)
    logits = jnp.dot(
        lax.all_gather(final_rows, "cand", axis=0, tiled=True),
        unembed,
        preferred_element_type=jnp.float32,
    )
    capped = 30.0 * jnp.tanh(logits / 30.0)
    totals = jnp.sum(jnp.exp(capped), axis=1)
    local_ids = targets - vocab_start
    matches = local_ids[:, None] == vocab_index[None, :]
    picked = jnp.sum(jnp.where(matches, capped, 0.0), axis=1)
    vocab_sums = jnp.stack([totals, picked], axis=0)
    summed_terms = lax.psum(vocab_sums, ("cand", "tensor"))
    own_terms = lax.dynamic_slice_in_dim(summed_terms, cand_id * length, length, 1)
    mask_values = loss_mask.astype(jnp.float32)
    token_loss = mask_values * (jnp.log(own_terms[0]) - own_terms[1])
    onehot = (chosen == jnp.arange(CANDS)).astype(jnp.float32)
    loss_sums, counts = lax.psum(
        (onehot * jnp.sum(token_loss), onehot * jnp.sum(mask_values)), "cand"
    )
    return (token_loss, loss_sums / jnp.maximum(counts, 1.0))


def solution(mesh):
    in_specs = (
        P("cand", None),
        P(),
        P("cand"),
        P(),
        P(),
        P("cand", "tensor"),
        P(None, "cand", "tensor"),
        P("cand", None),
        P(None, "cand", None),
        P("cand", None),
        P(None, "cand", None),
        P("tensor", "cand"),
        P(None, "tensor", "cand"),
        P(),
        P(),
        P(),
        P(None, ("cand", "tensor")),
    )
    out_specs = (P("cand"), P())
    return jax.shard_map(
        on_device, mesh=mesh, in_specs=in_specs, out_specs=out_specs, check_vma=False
    )
```

profile of v0, /device:TPU:0, one launch (start us, length us, event | category | flops | bytes accessed | tf_op | source)
XLA Modules:
  0.0 451.5 jit_solution(439209231556427896)
XLA Ops:
  7.2 0.0 copy-start.2
  7.2 0.0 all-gather.14.cloned.1.call-start
  7.2 1.9 constant_dynamic-slice_fusion.1
  9.2 0.0 all-gather.14.cloned.1.call-update
  9.2 0.0 all-gather.16.cloned.1.call-start
  9.2 2.3 dynamic-slice_reduce_fusion
  11.5 0.0 all-gather.16.cloned.1.call-update
  11.6 0.0 all-gather.20.cloned.1.call-start
  11.6 0.0 copy-done.2
  11.6 1.6 reduce_sum.123
  13.2 0.0 all-gather.20.cloned.1.call-update
  13.2 0.0 all-gather.18.cloned.1.call-start
  13.2 0.5 all-gather.18.cloned.1.call-update
  13.8 0.0 all-gather.10.cloned.1.call-start
  13.8 1.8 constant_dynamic-slice_fusion.2
  15.7 0.0 all-gather.10.cloned.1.call-update
  15.7 0.0 copy-start.8
  15.7 0.0 all-gather.12.cloned.1.call-start
  15.7 2.4 dynamic-slice_reduce_fusion.1
  18.1 0.0 all-gather.12.cloned.1.call-update
  18.2 0.0 all-gather.24.cloned.1.call-start
  18.2 1.5 reduce_sum.125
  19.7 0.0 all-gather.24.cloned.1.call-update
  19.7 0.0 all-gather.22.cloned.1.call-start
  19.8 0.7 all-gather.22.cloned.1.call-update
  20.5 0.0 all-reduce.3.cloned.1.call-start
  20.6 0.6 dynamic_slice.22
  23.1 0.6 dynamic_slice.23
  23.7 0.3 fusion.4
  24.0 0.3 multiply_cosine_fusion
  24.3 9.1 %all-gather.14.cloned.1.call-done = bf16[3584,256]{1,0:T(8,128)(2,1)} async-done(((bf16[896,256]{1,0:T(8,128)(2,1)}), bf16[3584,256]{1,0:T(8,128)(2,1)}) %all-gather.14.cloned.1.call-update) | async-done | bytes 1835024 | tf_op jit(solution)/shard_map/all_gather | solution.py:74
  33.4 22.7 %all-gather.16.cloned.1.call-done = bf16[3584,256]{1,0:T(8,128)(2,1)} async-done(((bf16[896,256]{1,0:T(8,128)(2,1)}), bf16[3584,256]{1,0:T(8,128)(2,1)}) %all-gather.16.cloned.1.call-update) | async-done | bytes 1835024 | tf_op jit(solution)/shard_map/all_gather | solution.py:78
  56.1 0.0 copy-done.8
  56.1 3.6 fusion.20
  59.7 0.3 fusion.37
  60.0 29.2 %all-gather.20.cloned.1.call-done = bf16[3584,512]{1,0:T(8,128)(2,1)} async-done(((bf16[896,512]{1,0:T(8,128)(2,1)}), bf16[3584,512]{1,0:T(8,128)(2,1)}) %all-gather.20.cloned.1.call-update) | async-done | bytes 3670032 | tf_op jit(solution)/shard_map/all_gather | solution.py:77
  89.2 32.9 %all-gather.18.cloned.1.call-done = bf16[3584,512]{1,0:T(8,128)(2,1)} async-done(((bf16[896,512]{1,0:T(8,128)(2,1)}), bf16[3584,512]{1,0:T(8,128)(2,1)}) %all-gather.18.cloned.1.call-update) | async-done | bytes 3670032 | tf_op jit(solution)/shard_map/all_gather | solution.py:73
  122.1 5.2 %fusion = f32[128,512]{1,0:T(8,128)S(1)} fusion(bf16[3584,512]{1,0:T(8,128)(2,1)} %all-gather.20.cloned.1.call-done, bf16[3584,512]{1,0:T(8,128)(2,1)} %all-gather.18.cloned.1.call-done, f32[]{:T(128)} %bitcast.1, bf16[128,3584]{1,0:T(8,128)(2,1)S(1)} %copy-done.1, f32[3584]{0:T(1024)S(1)} %copy-done.8, f32[128]{0:T(128)S(1)} %add_rsqrt_fusion.2), kind=kOutput, calls=%fused_computation.6 | convolution fusion | flops 480772096 | bytes 8534532 | tf_op jit(solution)/shard_map/dot_general | solution.py:91
  127.3 0.2 reshape.177
  127.5 0.1 fusion.53
  127.7 0.2 fusion.15
  127.9 16.7 %all-gather.10.cloned.1.call-done = bf16[3584,256]{1,0:T(8,128)(2,1)} async-done(((bf16[896,256]{1,0:T(8,128)(2,1)}), bf16[3584,256]{1,0:T(8,128)(2,1)}) %all-gather.10.cloned.1.call-update) | async-done | bytes 1835024 | tf_op jit(solution)/shard_map/all_gather | solution.py:75
  144.6 22.5 %all-gather.12.cloned.1.call-done = bf16[3584,256]{1,0:T(8,128)(2,1)} async-done(((bf16[896,256]{1,0:T(8,128)(2,1)}), bf16[3584,256]{1,0:T(8,128)(2,1)}) %all-gather.12.cloned.1.call-update) | async-done | bytes 1835024 | tf_op jit(solution)/shard_map/all_gather | solution.py:79
  167.2 3.9 convolution_convert_fusion
  171.1 29.1 %all-gather.24.cloned.1.call-done = bf16[512,3584]{1,0:T(8,128)(2,1)} async-done(((bf16[512,896]{1,0:T(8,128)(2,1)}), bf16[512,3584]{1,0:T(8,128)(2,1)}) %all-gather.24.cloned.1.call-update) | async-done | bytes 3670032 | tf_op jit(solution)/shard_map/all_gather | solution.py:80
  200.2 33.1 %all-gather.22.cloned.1.call-done = bf16[512,3584]{1,0:T(8,128)(2,1)} async-done(((bf16[512,896]{1,0:T(8,128)(2,1)}), bf16[512,3584]{1,0:T(8,128)(2,1)}) %all-gather.22.cloned.1.call-update) | async-done | bytes 3670032 | tf_op jit(solution)/shard_map/all_gather | solution.py:76
  233.3 6.6 %fusion.1 = f32[128,3584]{1,0:T(8,128)} fusion(bf16[128,512]{0,1:T(8,128)(2,1)S(1)} %bitcast.38, bf16[512,3584]{1,0:T(8,128)(2,1)} %all-gather.24.cloned.1.call-done, bf16[512,3584]{1,0:T(8,128)(2,1)} %all-gather.22.cloned.1.call-done, f32[]{:T(128)} %bitcast.1), kind=kOutput, calls=%fused_computation.7 | convolution fusion | flops 478937088 | bytes 9306116 | tf_op jit(solution)/shard_map/dot_general | solution.py:111
  239.9 0.0 all-reduce.3.cloned.1.call-update
  239.9 0.2 all-gather.26.cloned.1.call-start
  240.2 95.7 %all-reduce.3.cloned.1.call-done = f32[128,3584]{1,0:T(8,128)} async-done(((f32[128,3584]{1,0:T(8,128)}), f32[128,3584]{1,0:T(8,128)}) %all-reduce.3.cloned.1.call-update) | async-done | bytes 1835024 | tf_op jit(solution)/shard_map/psum | solution.py:115
  335.9 1.8 multiply_reduce_fusion.1
  337.8 0.0 copy-done.4
  337.8 0.0 copy-start.6
  337.8 2.0 multiply_reduce_fusion
  339.8 1.4 multiply_convert_fusion
  341.2 0.0 all-gather.26.cloned.1.call-update
  341.3 0.0 copy-start.7
  341.3 31.1 %all-gather.26.cloned.1.call-done = bf16[512,3584]{1,0:T(8,128)(2,1)} async-done(((bf16[128,3584]{1,0:T(8,128)(2,1)}), bf16[512,3584]{1,0:T(8,128)(2,1)}) %all-gather.26.cloned.1.call-update) | async-done | bytes 3670032 | tf_op jit(solution)/shard_map/all_gather | solution.py:118
  372.4 22.9 %exponential_reduce_fusion = (f32[512]{0:T(512)S(1)}, f32[512]{0:T(512)S(1)}) fusion(s32[512]{0:T(512)S(1)} %broadcast_subtract_fusion, bf16[512,3584]{1,0:T(8,128)(2,1)} %all-gather.26.cloned.1.call-done, bf16[3584,4096]{1,0:T(8,128)(2,1)} %param.33), kind=kOutput, calls=%fused_computation.2 | convolution fusion | flops 15044968448 | bytes 33036288 | tf_op jit(solution)/shard_map/dot_general | solution.py:117
  395.3 39.3 %psum.29 = f32[2,512]{1,0:T(2,128)S(1)} all-reduce(f32[2,512]{1,0:T(2,128)S(1)} %pad_maximum_fusion), channel_id=1, replica_groups=mesh['cand'=4,'tensor'=8] {'cand','tensor'}, use_global_device_ids=true, to_apply=%region_11.12 | all-reduce | flops 1024 | bytes 8192 | tf_op jit(solution)/shard_map/psum | solution.py:128
  434.7 1.1 fusion.52
  435.8 1.8 compare_select_fusion
  437.6 6.5 %all-reduce = (f32[4]{0:T(128)S(1)}, f32[4]{0:T(128)S(1)}) all-reduce(f32[4]{0:T(128)S(1)} %get-tuple-element.18, f32[4]{0:T(128)S(1)} %get-tuple-element.17), channel_id=1, replica_groups=mesh['cand'=4,'tensor'=8] {'cand'}, use_global_device_ids=true, to_apply=%region_13.14 | all-reduce | flops 8 | bytes 64 | tf_op jit(solution)/shard_map/psum | solution.py:133
  444.2 0.5 maximum_divide_fusion
  (25 shorter events, 0.1 us)
Async XLA Ops:
  7.2 4.4 copy-start.2
  7.2 26.2 %all-gather.14.cloned.1.call-start = ((), (), s32[]{:S(2)}) async-start(), calls=%async_computation.2 | async-start | bytes 2293760 | tf_op jit(solution)/shard_map/all_gather | solution.py:74
  9.2 46.9 %all-gather.16.cloned.1.call-start = ((), (), s32[]{:S(2)}) async-start(), calls=%async_computation.3 | async-start | bytes 2293760 | tf_op jit(solution)/shard_map/all_gather | solution.py:78
  11.6 77.6 %all-gather.20.cloned.1.call-start = ((), (), s32[]{:S(2)}) async-start(), calls=%async_computation.5 | async-start | bytes 4587520 | tf_op jit(solution)/shard_map/all_gather | solution.py:77
  13.2 5.0 %copy-start.3 = (bf16[2,512,896]{2,1,0:T(8,128)(2,1)S(1)}, bf16[2,512,896]{2,1,0:T(8,128)(2,1)}, u32[]{:S(2)}) copy-start(bf16[2,512,896]{2,1,0:T(8,128)(2,1)} %param.29) | copy-start | bytes 5505028
  13.2 108.9 %all-gather.18.cloned.1.call-start = ((), (), s32[]{:S(2)}) async-start(), calls=%async_computation.4 | async-start | bytes 4587520 | tf_op jit(solution)/shard_map/all_gather | solution.py:73
  13.8 130.9 %all-gather.10.cloned.1.call-start = ((), (), s32[]{:S(2)}) async-start(), calls=%async_computation | async-start | bytes 2293760 | tf_op jit(solution)/shard_map/all_gather | solution.py:75
  15.6 4.9 %copy-start.9 = (s32[4]{0:T(128)S(1)}, s32[4]{0:T(128)}, u32[]{:S(2)}) copy-start(s32[4]{0:T(128)} %param.20) | copy-start | bytes 52
  15.6 7.4 %copy-start.10 = (f32[4]{0:T(128)S(1)}, f32[4]{0:T(128)}, u32[]{:S(2)}) copy-start(f32[4]{0:T(128)} %param.21) | copy-start | bytes 52
  15.7 8.1 %copy-start.1 = (bf16[128,3584]{1,0:T(8,128)(2,1)S(1)}, bf16[128,3584]{1,0:T(8,128)(2,1)}, u32[]{:S(2)}) copy-start(bf16[128,3584]{1,0:T(8,128)(2,1)} %param.17) | copy-start | bytes 2752516
  15.7 40.4 %copy-start.8 = (f32[3584]{0:T(1024)S(1)}, f32[3584]{0:T(1024)}, u32[]{:S(2)}) copy-start(f32[3584]{0:T(1024)} %param.30) | copy-start | bytes 43012
  15.7 151.5 %all-gather.12.cloned.1.call-start = ((), (), s32[]{:S(2)}) async-start(), calls=%async_computation.1 | async-start | bytes 2293760 | tf_op jit(solution)/shard_map/all_gather | solution.py:79
  18.2 182.1 %all-gather.24.cloned.1.call-start = ((), (), s32[]{:S(2)}) async-start(), calls=%async_computation.7 | async-start | bytes 4587520 | tf_op jit(solution)/shard_map/all_gather | solution.py:80
  19.7 213.6 %all-gather.22.cloned.1.call-start = ((), (), s32[]{:S(2)}) async-start(), calls=%async_computation.6 | async-start | bytes 4587520 | tf_op jit(solution)/shard_map/all_gather | solution.py:76
  20.5 315.4 %all-reduce.3.cloned.1.call-start = ((), (), s32[]{:S(2)}) async-start(), calls=%async_computation.8 | async-start | bytes 3670016 | tf_op jit(solution)/shard_map/psum | solution.py:115
  239.9 97.8 %copy-start.4 = (f32[3584]{0:T(1024)S(1)}, f32[3584]{0:T(1024)}, u32[]{:S(2)}) copy-start(f32[3584]{0:T(1024)} %param.31) | copy-start | bytes 43012
  239.9 99.9 %copy-start.5 = (f32[3584]{0:T(1024)S(1)}, f32[3584]{0:T(1024)}, u32[]{:S(2)}) copy-start(f32[3584]{0:T(1024)} %param.32) | copy-start | bytes 43012
  239.9 132.5 %all-gather.26.cloned.1.call-start = ((), (), s32[]{:S(2)}) async-start(), calls=%async_computation.9 | async-start | bytes 4587520 | tf_op jit(solution)/shard_map/all_gather | solution.py:118
  335.9 3.9 copy-start
  337.8 3.5 copy-start.6
  341.3 93.4 %copy-start.7 = (s32[128]{0:T(128)S(1)}, s32[128]{0:T(128)}, u32[]{:S(2)}) copy-start(s32[128]{0:T(128)} %param.19) | copy-start | bytes 1540
Sparse Core Ops, SparseCore 0:
  9.5 23.8 all-gather.13
  35.0 21.0 all-gather.15
  57.7 31.4 all-gather.19
  90.6 31.4 all-gather.17
  123.5 21.0 all-gather.9
  146.1 21.0 all-gather.11
  168.7 31.4 all-gather.23
  201.8 31.4 all-gather.21
  240.1 95.7 all-reduce.2
  341.4 30.9 all-gather.25
where the time goes:
time: 452 us
  waiting for transfers between devices  324 us (72%)
  blocking collectives  45.9 us (10%)
  matrix products  42.5 us (9%)
  other arithmetic  17.5 us (4%)
  between operations  16.3 us (4%)
  local copies, waits for them, and re-layouts  5.26 us (1%)
    psum x1, waiting for transfers between devices, on_device(): attended = lax.psum(partial_value, 'tensor')  95.7 us
    psum x1, blocking collectives, on_device(): summed_terms = lax.psum(vocab_sums, ('cand', 'tensor'))  39.3 us
    all_gather x1, waiting for transfers between devices, on_device(): lax.all_gather(base_o, 'cand', axis=1, tiled=True)  33.1 us
    all_gather x1, waiting for transfers between devices, on_device(): lax.all_gather(base_q, 'cand', axis=0, tiled=True)  32.9 us
    all_gather x1, waiting for transfers between devices, on_device(): lax.all_gather(final_rows, 'cand', axis=0, tiled=True)  31.1 us
    all_gather x1, waiting for transfers between devices, on_device(): lax.all_gather(summed[0], 'cand', axis=0, tiled=True)  29.2 us
    all_gather x1, waiting for transfers between devices, on_device(): lax.all_gather(summed[3], 'cand', axis=1, tiled=True)  29.1 us
    dot_general x1, matrix products, on_device(): jnp.dot(lax.all_gather(final_rows, 'cand', axis=0, tiled=True), unembed,...  22.9 us
  transfers between devices with their start and end apart: 10, of which 10 were waited for; matrix products, arithmetic and copies ran while one was open for 6% of the time, Pallas kernels for 0%

commit v1 on v0

--- a/solution.py
+++ b/solution.py
@@ -7,6 +7,12 @@
 KV = 8
 HEAD_SIZE = 256
 CANDS = 4
+
+
+def all_parts(x, axis, d):
+    blocks = lax.all_gather(x, axis, axis=0, tiled=False)
+    whole = jnp.concatenate(blocks, axis=d)
+    return whole
 
 
 def root_norm(entries, scale_gain):
@@ -73,7 +79,7 @@
         lax.all_gather(base_q, "cand", axis=0, tiled=True),
         lax.all_gather(own_base_k, "cand", axis=0, tiled=True),
         lax.all_gather(own_base_v, "cand", axis=0, tiled=True),
-        lax.all_gather(base_o, "cand", axis=1, tiled=True),
+        all_parts(base_o, "cand", 1),
         lax.all_gather(summed[0], "cand", axis=0, tiled=True),
         lax.all_gather(summed[1], "cand", axis=0, tiled=True),
         lax.all_gather(summed[2], "cand", axis=0, tiled=True),

time: 452 us -> 453 us (level)
  waiting for transfers between devices: 324 us -> 302 us
  local copies, waits for them, and re-layouts: 5.26 us -> 22 us
  other arithmetic: 17.5 us -> 22.8 us
    all_gather x1, waiting for transfers between devices: 16.7 us -> 0.11 us  [on_device(): lax.all_gather(own_base_v, 'cand', axis=0, tiled=True)]
    convert_element_type x0 -> x2, local copies, waits for them, and re-layouts: none -> 16.6 us  [merge_weights(): base.astype(jnp.float32) + mixing * total.astype(jnp.float32)]
    all_gather x1, waiting for transfers between devices: 33.1 us -> 27.5 us  [all_parts(): blocks = lax.all_gather(x, axis, axis=0, tiled=False)]
    convert_element_type x0 -> x1, other arithmetic: none -> 5.46 us  [merge_weights(): base.astype(jnp.float32) + mixing * total.astype(jnp.float32)]
  transfers between devices with their start and end apart: 10 -> 10, of which waited for: 10 -> 10; matrix products, arithmetic and copies ran while one was open for 6% -> 10% of each run, Pallas kernels for 0% -> 0%
where the time goes in v1:
time: 453 us; the launch traced here: 452 us
  waiting for transfers between devices  302 us (67%)
  blocking collectives  45.9 us (10%)
  matrix products  43.1 us (10%)
  other arithmetic  22.8 us (5%)
  local copies, waits for them, and re-layouts  22 us (5%)
  between operations  16.3 us (4%)
    psum x1, waiting for transfers between devices, on_device(): attended = lax.psum(partial_value, 'tensor')  95.7 us
    psum x1, blocking collectives, on_device(): summed_terms = lax.psum(vocab_sums, ('cand', 'tensor'))  39.3 us
    all_gather x1, waiting for transfers between devices, on_device(): lax.all_gather(base_q, 'cand', axis=0, tiled=True)  32.9 us
    all_gather x1, waiting for transfers between devices, on_device(): lax.all_gather(final_rows, 'cand', axis=0, tiled=True)  31.1 us
    all_gather x1, waiting for transfers between devices, on_device(): lax.all_gather(summed[3], 'cand', axis=1, tiled=True)  29.3 us
    all_gather x1, waiting for transfers between devices, on_device(): lax.all_gather(summed[0], 'cand', axis=0, tiled=True)  29.2 us
    all_gather x1, waiting for transfers between devices, all_parts(): blocks = lax.all_gather(x, axis, axis=0, tiled=False)  27.5 us
    dot_general x1, matrix products, on_device(): jnp.dot(lax.all_gather(final_rows, 'cand', axis=0, tiled=True), unembed,...  22.9 us
  transfers between devices with their start and end apart: 10, of which 10 were waited for; matrix products, arithmetic and copies ran while one was open for 10% of the time, Pallas kernels for 0%

profile of v1, /device:TPU:0, one launch (start us, length us, event | category | flops | bytes accessed | tf_op | source)
XLA Modules:
  0.0 452.3 jit_solution(3293540329479006012)
XLA Ops:
  7.2 0.0 all-gather.15.cloned.1.call-start
  7.2 2.0 constant_dynamic-slice_fusion.1
  9.2 0.0 all-gather.15.cloned.1.call-update
  9.3 0.0 all-gather.17.cloned.1.call-start
  9.3 2.3 dynamic-slice_reduce_fusion
  11.6 0.0 all-gather.17.cloned.1.call-update
  11.6 0.0 all-gather.21.cloned.1.call-start
  11.7 1.5 reduce_sum.123
  13.2 0.0 all-gather.21.cloned.1.call-update
  13.2 0.0 all-gather.19.cloned.1.call-start
  13.2 0.5 all-gather.19.cloned.1.call-update
  13.8 0.0 all-gather.27.cloned.1.call-start
  13.8 0.5 all-gather.27.cloned.1.call-update
  14.4 0.0 copy-start.9
  14.4 0.0 copy-start.10
  14.4 0.0 copy-start.1
  14.4 0.0 all-gather.11.cloned.1.call-start
  14.4 1.9 constant_dynamic-slice_fusion.2
  16.3 0.0 all-gather.11.cloned.1.call-update
  16.4 0.0 all-gather.13.cloned.1.call-start
  16.4 2.2 dynamic-slice_reduce_fusion.1
  18.7 0.0 all-gather.13.cloned.1.call-update
  18.7 0.0 all-gather.23.cloned.1.call-start
  18.7 1.6 reduce_sum.125
  20.3 0.0 all-gather.23.cloned.1.call-update
  20.3 0.0 all-reduce.3.cloned.1.call-start
  20.4 0.6 dynamic_slice.22
  22.9 0.6 dynamic_slice.23
  23.6 0.3 fusion.4
  23.8 0.3 multiply_cosine_fusion
  24.1 9.3 %all-gather.15.cloned.1.call-done = bf16[3584,256]{1,0:T(8,128)(2,1)} async-done(((bf16[896,256]{1,0:T(8,128)(2,1)}), bf16[3584,256]{1,0:T(8,128)(2,1)}) %all-gather.15.cloned.1.call-update) | async-done | bytes 1835024 | tf_op jit(solution)/shard_map/all_gather | solution.py:80
  33.4 22.7 %all-gather.17.cloned.1.call-done = bf16[3584,256]{1,0:T(8,128)(2,1)} async-done(((bf16[896,256]{1,0:T(8,128)(2,1)}), bf16[3584,256]{1,0:T(8,128)(2,1)}) %all-gather.17.cloned.1.call-update) | async-done | bytes 1835024 | tf_op jit(solution)/shard_map/all_gather | solution.py:84
  56.1 3.6 fusion.20
  59.7 0.3 fusion.37
  60.0 29.2 %all-gather.21.cloned.1.call-done = bf16[3584,512]{1,0:T(8,128)(2,1)} async-done(((bf16[896,512]{1,0:T(8,128)(2,1)}), bf16[3584,512]{1,0:T(8,128)(2,1)}) %all-gather.21.cloned.1.call-update) | async-done | bytes 3670032 | tf_op jit(solution)/shard_map/all_gather | solution.py:83
  89.2 32.9 %all-gather.19.cloned.1.call-done = bf16[3584,512]{1,0:T(8,128)(2,1)} async-done(((bf16[896,512]{1,0:T(8,128)(2,1)}), bf16[3584,512]{1,0:T(8,128)(2,1)}) %all-gather.19.cloned.1.call-update) | async-done | bytes 3670032 | tf_op jit(solution)/shard_map/all_gather | solution.py:79
  122.1 5.2 %fusion = f32[128,512]{1,0:T(8,128)S(1)} fusion(bf16[3584,512]{1,0:T(8,128)(2,1)} %all-gather.21.cloned.1.call-done, bf16[3584,512]{1,0:T(8,128)(2,1)} %all-gather.19.cloned.1.call-done, f32[]{:T(128)} %bitcast.1, bf16[128,3584]{1,0:T(8,128)(2,1)S(1)} %copy-done.1, f32[3584]{0:T(1024)S(1)} %copy-done.8, f32[128]{0:T(128)S(1)} %add_rsqrt_fusion.2), kind=kOutput, calls=%fused_computation.7 | convolution fusion | flops 480772096 | bytes 8534532 | tf_op jit(solution)/shard_map/dot_general | solution.py:97
  127.3 0.2 reshape.181
  127.5 27.5 %all-gather.27.cloned.1.call-done = bf16[2048,896]{1,0:T(8,128)(2,1)} async-done(((bf16[512,896]{1,0:T(8,128)(2,1)}), bf16[2048,896]{1,0:T(8,128)(2,1)}) %all-gather.27.cloned.1.call-update) | async-done | bytes 3670032 | tf_op jit(solution)/shard_map/all_gather | solution.py:13
  155.0 5.5 %convert_bitcast_fusion = f32[512,4,896]{2,0,1:T(8,128)} fusion(bf16[4,512,896]{2,1,0:T(8,128)(2,1)} %bitcast.44), kind=kLoop, calls=%fused_computation.4 | loop fusion | flops 1835008 | bytes 11010048 | tf_op jit(solution)/shard_map/convert_element_type | solution.py:44
  160.5 8.2 %copy.34 = f32[512,4,896]{0,2,1:T(8,128)} copy(f32[512,4,896]{2,0,1:T(8,128)} %convert_bitcast_fusion) | data formatting | bytes 14680064 | tf_op jit(solution)/shard_map/convert_element_type | solution.py:44
  168.7 8.4 %copy.35 = f32[512,3584]{1,0:T(8,128)} copy(f32[512,3584]{0,1:T(8,128)} %bitcast.43) | data formatting | bytes 14680064 | tf_op jit(solution)/shard_map/convert_element_type | solution.py:44
  177.1 0.1 fusion.53
  177.2 0.2 fusion.15
  177.5 0.1 all-gather.11.cloned.1.call-done
  177.6 22.7 %all-gather.13.cloned.1.call-done = bf16[3584,256]{1,0:T(8,128)(2,1)} async-done(((bf16[896,256]{1,0:T(8,128)(2,1)}), bf16[3584,256]{1,0:T(8,128)(2,1)}) %all-gather.13.cloned.1.call-update) | async-done | bytes 1835024 | tf_op jit(solution)/shard_map/all_gather | solution.py:85
  200.3 3.8 convolution_convert_fusion
  204.1 29.3 %all-gather.23.cloned.1.call-done = bf16[512,3584]{1,0:T(8,128)(2,1)} async-done(((bf16[512,896]{1,0:T(8,128)(2,1)}), bf16[512,3584]{1,0:T(8,128)(2,1)}) %all-gather.23.cloned.1.call-update) | async-done | bytes 3670032 | tf_op jit(solution)/shard_map/all_gather | solution.py:86
  233.4 7.3 %fusion.1 = f32[128,3584]{1,0:T(8,128)} fusion(bf16[128,512]{0,1:T(8,128)(2,1)S(1)} %bitcast.45, f32[512,3584]{1,0:T(8,128)} %copy.35, bf16[512,3584]{1,0:T(8,128)(2,1)} %all-gather.23.cloned.1.call-done, f32[]{:T(128)} %bitcast.1), kind=kOutput, calls=%fused_computation.8 | convolution fusion | flops 477102080 | bytes 12976132 | tf_op jit(solution)/shard_map/dot_general | solution.py:117
  240.7 0.0 all-reduce.3.cloned.1.call-update
  240.7 0.2 all-gather.25.cloned.1.call-start
  241.0 95.7 %all-reduce.3.cloned.1.call-done = f32[128,3584]{1,0:T(8,128)} async-done(((f32[128,3584]{1,0:T(8,128)}), f32[128,3584]{1,0:T(8,128)}) %all-reduce.3.cloned.1.call-update) | async-done | bytes 1835024 | tf_op jit(solution)/shard_map/psum | solution.py:121
  336.7 1.8 multiply_reduce_fusion.1
  338.6 0.0 copy-start.6
  338.6 2.0 multiply_reduce_fusion
  340.6 1.4 multiply_convert_fusion
  342.0 0.0 all-gather.25.cloned.1.call-update
  342.1 31.1 %all-gather.25.cloned.1.call-done = bf16[512,3584]{1,0:T(8,128)(2,1)} async-done(((bf16[128,3584]{1,0:T(8,128)(2,1)}), bf16[512,3584]{1,0:T(8,128)(2,1)}) %all-gather.25.cloned.1.call-update) | async-done | bytes 3670032 | tf_op jit(solution)/shard_map/all_gather | solution.py:124
  373.2 22.9 %exponential_reduce_fusion = (f32[512]{0:T(512)S(1)}, f32[512]{0:T(512)S(1)}) fusion(s32[512]{0:T(512)S(1)} %broadcast_subtract_fusion, bf16[512,3584]{1,0:T(8,128)(2,1)} %all-gather.25.cloned.1.call-done, bf16[3584,4096]{1,0:T(8,128)(2,1)} %param.33), kind=kOutput, calls=%fused_computation.2 | convolution fusion | flops 15044968448 | bytes 33036288 | tf_op jit(solution)/shard_map/dot_general | solution.py:123
  396.1 39.3 %psum.29 = f32[2,512]{1,0:T(2,128)S(1)} all-reduce(f32[2,512]{1,0:T(2,128)S(1)} %pad_maximum_fusion), channel_id=1, replica_groups=mesh['cand'=4,'tensor'=8] {'cand','tensor'}, use_global_device_ids=true, to_apply=%region_11.12 | all-reduce | flops 1024 | bytes 8192 | tf_op jit(solution)/shard_map/psum | solution.py:134
  435.5 1.1 fusion.52
  436.6 1.8 compare_select_fusion
  438.4 6.5 %all-reduce = (f32[4]{0:T(128)S(1)}, f32[4]{0:T(128)S(1)}) all-reduce(f32[4]{0:T(128)S(1)} %get-tuple-element.18, f32[4]{0:T(128)S(1)} %get-tuple-element.17), channel_id=1, replica_groups=mesh['cand'=4,'tensor'=8] {'cand'}, use_global_device_ids=true, to_apply=%region_13.14 | all-reduce | flops 8 | bytes 64 | tf_op jit(solution)/shard_map/psum | solution.py:139
  445.0 0.5 maximum_divide_fusion
  (28 shorter events, 0.2 us)
Async XLA Ops:
  7.2 4.5 copy-start.2
  7.2 26.2 %all-gather.15.cloned.1.call-start = ((), (), s32[]{:S(2)}) async-start(), calls=%async_computation.2 | async-start | bytes 2293760 | tf_op jit(solution)/shard_map/all_gather | solution.py:80
  9.3 46.8 %all-gather.17.cloned.1.call-start = ((), (), s32[]{:S(2)}) async-start(), calls=%async_computation.3 | async-start | bytes 2293760 | tf_op jit(solution)/shard_map/all_gather | solution.py:84
  11.6 77.6 %all-gather.21.cloned.1.call-start = ((), (), s32[]{:S(2)}) async-start(), calls=%async_computation.5 | async-start | bytes 4587520 | tf_op jit(solution)/shard_map/all_gather | solution.py:83
  13.2 5.6 %copy-start.3 = (bf16[2,512,896]{2,1,0:T(8,128)(2,1)S(1)}, bf16[2,512,896]{2,1,0:T(8,128)(2,1)}, u32[]{:S(2)}) copy-start(bf16[2,512,896]{2,1,0:T(8,128)(2,1)} %param.29) | copy-start | bytes 5505028
  13.2 108.9 %all-gather.19.cloned.1.call-start = ((), (), s32[]{:S(2)}) async-start(), calls=%async_computation.4 | async-start | bytes 4587520 | tf_op jit(solution)/shard_map/all_gather | solution.py:79
  13.8 141.2 %all-gather.27.cloned.1.call-start = ((), (), s32[]{:S(2)}) async-start(), calls=%async_computation.9 | async-start | bytes 4587520 | tf_op jit(solution)/shard_map/all_gather | solution.py:13
  14.4 6.0 %copy-start.9 = (s32[4]{0:T(128)S(1)}, s32[4]{0:T(128)}, u32[]{:S(2)}) copy-start(s32[4]{0:T(128)} %param.20) | copy-start | bytes 52
  14.4 8.5 %copy-start.10 = (f32[4]{0:T(128)S(1)}, f32[4]{0:T(128)}, u32[]{:S(2)}) copy-start(f32[4]{0:T(128)} %param.21) | copy-start | bytes 52
  14.4 9.2 %copy-start.1 = (bf16[128,3584]{1,0:T(8,128)(2,1)S(1)}, bf16[128,3584]{1,0:T(8,128)(2,1)}, u32[]{:S(2)}) copy-start(bf16[128,3584]{1,0:T(8,128)(2,1)} %param.17) | copy-start | bytes 2752516
  14.4 163.2 %all-gather.11.cloned.1.call-start = ((), (), s32[]{:S(2)}) async-start(), calls=%async_computation | async-start | bytes 2293760 | tf_op jit(solution)/shard_map/all_gather | solution.py:81
  16.3 39.7 %copy-start.8 = (f32[3584]{0:T(1024)S(1)}, f32[3584]{0:T(1024)}, u32[]{:S(2)}) copy-start(f32[3584]{0:T(1024)} %param.30) | copy-start | bytes 43012
  16.4 183.9 %all-gather.13.cloned.1.call-start = ((), (), s32[]{:S(2)}) async-start(), calls=%async_computation.1 | async-start | bytes 2293760 | tf_op jit(solution)/shard_map/all_gather | solution.py:85
  18.7 214.7 %all-gather.23.cloned.1.call-start = ((), (), s32[]{:S(2)}) async-start(), calls=%async_computation.6 | async-start | bytes 4587520 | tf_op jit(solution)/shard_map/all_gather | solution.py:86
  20.3 316.4 %all-reduce.3.cloned.1.call-start = ((), (), s32[]{:S(2)}) async-start(), calls=%async_computation.7 | async-start | bytes 3670016 | tf_op jit(solution)/shard_map/psum | solution.py:121
  240.7 97.9 %copy-start.4 = (f32[3584]{0:T(1024)S(1)}, f32[3584]{0:T(1024)}, u32[]{:S(2)}) copy-start(f32[3584]{0:T(1024)} %param.31) | copy-start | bytes 43012
  240.7 99.9 %copy-start.5 = (f32[3584]{0:T(1024)S(1)}, f32[3584]{0:T(1024)}, u32[]{:S(2)}) copy-start(f32[3584]{0:T(1024)} %param.32) | copy-start | bytes 43012
  240.7 132.5 %all-gather.25.cloned.1.call-start = ((), (), s32[]{:S(2)}) async-start(), calls=%async_computation.8 | async-start | bytes 4587520 | tf_op jit(solution)/shard_map/all_gather | solution.py:124
  336.7 3.9 copy-start
  338.6 3.5 copy-start.6
  342.1 93.4 %copy-start.7 = (s32[128]{0:T(128)S(1)}, s32[128]{0:T(128)}, u32[]{:S(2)}) copy-start(s32[128]{0:T(128)} %param.19) | copy-start | bytes 1540
Sparse Core Ops, SparseCore 0:
  9.5 23.8 all-gather.14
  35.0 21.0 all-gather.16
  57.7 31.4 all-gather.20
  90.6 31.4 all-gather.18
  123.5 31.4 all-gather.26
  156.4 21.0 all-gather.10
  179.1 21.1 all-gather.12
  201.9 31.4 all-gather.22
  240.8 95.7 all-reduce.2
  342.2 30.9 all-gather.24
